TPU v7x, 32 devices: a whole 2x2x4 slice. The times are simulated.
32 devices in a mesh: group: 2 (over core), row: 2 (over x), col: 8 (over z, y).
Axes of the slice: x: 2, y: 2, z: 4, core: 2. Of those that a mesh axis runs over, the one named last changes fastest.
Arguments:
- velocity_hat: float32 [3, 2, 4, 512, 512], P(None, None, ('group', 'row'), 'col'), may hold values from -6 to 6
- scalar: float32 [4, 1024, 1024], P('group', 'col', 'row'), may hold values from -6 to 6
- tile_offset: int32 [1], replicated, may hold values from 0 to 511
Outputs:
- velocity_new: float32 [3, 2, 4, 512, 512], P(None, None, ('group', 'row'), 'col')
- scalar_new: float32 [4, 1024, 1024], P('group', 'col', 'row')
Inputs may be any that keep to these rules, and one draw needn't show every extreme that they name: `tile_offset`: one offset for every tile and plane.
All inputs are finite; a program needn't handle non-finite values.
Results may differ from a plain program's by a relative error of at most 0.000076.
Values sent between devices are 32-bit elements; how exact they have to be, the bound alone decides.
No kernel may reach another device: no remote copies, remote signals or barrier semaphores. Data moves between devices by JAX's collectives and lax.ppermute only.
A program may use at most 64 MiB of HBM per device.

v0:
```python
import functools
import itertools
import math

import jax
import jax.numpy as jnp
import numpy as np
from jax import lax
from jax.experimental import pallas as pl
from jax.experimental.pallas import tpu as pltpu
from jax.sharding import PartitionSpec as P


time_step = 0.25
viscosity = 2.0
diffusivity = 0.15
substep = 0.2
highest = lax.Precision.HIGHEST


def extended(cells, sides, width):
    for axis, dim in sides:
        count = lax.axis_size(axis)
        head = lax.slice_in_dim(cells, 0, width, axis=dim)
        tail = lax.slice_in_dim(cells, cells.shape[dim] - width, cells.shape[dim], axis=dim)
        cells = jnp.concatenate(
            [
                lax.ppermute(tail, axis, [(i, (i + 1) % count) for i in range(count)]),
                cells,
                lax.ppermute(head, axis, [((i + 1) % count, i) for i in range(count)]),
            ],
            axis=dim,
        )
    return cells


def dft_tables(length):
    indices = jnp.arange(length, dtype=jnp.int32)
    phases = indices[:, None] * indices[None, :] % length
    angles = phases.astype(jnp.float32) * (2.0 * math.pi / length)
    factor = 1.0 / math.sqrt(length)
    return (jnp.cos(angles) * factor, jnp.sin(angles) * factor)


def signed_wave(indices, length):
    return jnp.where(indices < length // 2, indices, indices - length)


def transpose_col(packed):
    return lax.all_to_all(packed, "col", split_axis=3, concat_axis=4, tiled=True)


def refine_rows(coarse, margin):
    current = coarse[:, :-1, :]
    following = coarse[:, 1:, :]
    paired = jnp.stack([current, (current + following) * 0.5], axis=2)
    refined = paired.reshape(coarse.shape[0], 2 * (coarse.shape[1] - 1), coarse.shape[2])
    height = 2 * (coarse.shape[1] - 2 * margin)
    return refined[:, margin : margin + height + 2 * margin, :]


def advance(values, x_speed, y_speed):
    height = values.shape[1] - 4
    breadth = values.shape[2] - 4

    def neighbor(step_y, step_x):
        return values[:, 2 + step_y : 2 + step_y + height, 2 + step_x : 2 + step_x + breadth]

    center = neighbor(0, 0)
    grad_x = (neighbor(0, -2) - neighbor(0, 2) + 8.0 * (neighbor(0, 1) - neighbor(0, -1))) / 12.0
    grad_y = (neighbor(-2, 0) - neighbor(2, 0) + 8.0 * (neighbor(1, 0) - neighbor(-1, 0))) / 12.0
    lap_x = (
        16.0 * (neighbor(0, 1) + neighbor(0, -1)) - neighbor(0, 2) - neighbor(0, -2) - 30.0 * center
    ) / 12.0
    lap_y = (
        16.0 * (neighbor(1, 0) + neighbor(-1, 0)) - neighbor(2, 0) - neighbor(-2, 0) - 30.0 * center
    ) / 12.0
    return center + substep * (
        diffusivity * (lap_x + lap_y) - (x_speed * grad_x + y_speed * grad_y)
    )


def per_device(velocity_hat, scalar, tile_offset):
    extent = velocity_hat.shape[4]
    kx_block = velocity_hat.shape[3]
    cosine_table, sine_table = dft_tables(extent)
    wave_all = signed_wave(jnp.arange(extent, dtype=jnp.int32), extent)
    local_wave = signed_wave(
        lax.axis_index("col") * kx_block + jnp.arange(kx_block, dtype=jnp.int32), extent
    )
    kappa_y = (wave_all.astype(jnp.float32) / (extent // 2))[None, None, :]
    kappa_x = (local_wave.astype(jnp.float32) / (extent // 2))[None, :, None]
    real_part = velocity_hat[:, 0]
    imag_part = velocity_hat[:, 1]
    spin_x_real = -kappa_y * imag_part[2]
    spin_x_imag = kappa_y * real_part[2]
    spin_z_real = kappa_y * imag_part[0] - kappa_x * imag_part[1]
    spin_z_imag = kappa_x * real_part[1] - kappa_y * real_part[0]
    fields_real = jnp.concatenate([real_part, jnp.stack([spin_x_real, spin_z_real])])
    fields_imag = jnp.concatenate([imag_part, jnp.stack([spin_x_imag, spin_z_imag])])
    lines_real = jnp.einsum(
        "fpkq,qy->fpyk", fields_real, cosine_table, precision=highest
    ) - jnp.einsum("fpkq,qy->fpyk", fields_imag, sine_table, precision=highest)
    lines_imag = jnp.einsum(
        "fpkq,qy->fpyk", fields_real, sine_table, precision=highest
    ) + jnp.einsum("fpkq,qy->fpyk", fields_imag, cosine_table, precision=highest)
    landed = transpose_col(jnp.stack([lines_real, lines_imag], axis=1))
    landed_real = landed[:, 0]
    landed_imag = landed[:, 1]
    wave_x = (wave_all.astype(jnp.float32) / (extent // 2))[None, None, :]
    spin_y_real = wave_x * landed_imag[2]
    spin_y_imag = -wave_x * landed_real[2]
    landed_real = jnp.concatenate([landed_real[:4], spin_y_real[None], landed_real[4:]])
    landed_imag = jnp.concatenate([landed_imag[:4], spin_y_imag[None], landed_imag[4:]])
    physical = jnp.einsum(
        "fpyk,kx->fpyx", landed_real, cosine_table, precision=highest
    ) - jnp.einsum("fpyk,kx->fpyx", landed_imag, sine_table, precision=highest)
    x_speed = physical[0]
    y_speed = physical[1]
    z_speed = physical[2]
    omega_x = physical[3]
    omega_y = physical[4]
    omega_z = physical[5]
    product = jnp.stack(
        [
            y_speed * omega_z - z_speed * omega_y,
            z_speed * omega_x - x_speed * omega_z,
            x_speed * omega_y - y_speed * omega_x,
        ]
    )
    rows_real = jnp.einsum("cpyx,xk->cpky", product, cosine_table, precision=highest)
    rows_imag = -jnp.einsum("cpyx,xk->cpky", product, sine_table, precision=highest)
    returned = transpose_col(jnp.stack([rows_real, rows_imag], axis=1))
    back_real = returned[:, 0]
    back_imag = returned[:, 1]
    forcing_real = jnp.einsum(
        "cpky,yq->cpkq", back_real, cosine_table, precision=highest
    ) + jnp.einsum("cpky,yq->cpkq", back_imag, sine_table, precision=highest)
    forcing_imag = jnp.einsum(
        "cpky,yq->cpkq", back_imag, cosine_table, precision=highest
    ) - jnp.einsum("cpky,yq->cpkq", back_real, sine_table, precision=highest)
    retained = (3 * jnp.abs(local_wave)[:, None] < extent) & (
        3 * jnp.abs(wave_all)[None, :] < extent
    )
    damping = jnp.exp(-viscosity * time_step * (kappa_x**2 + kappa_y**2))
    new_real = damping * (real_part + time_step * jnp.where(retained, forcing_real, 0.0))
    new_imag = damping * (imag_part + time_step * jnp.where(retained, forcing_imag, 0.0))
    velocity_new = jnp.stack([new_real, new_imag], axis=1)
    horizontal = physical[:2]
    doubled = jnp.concatenate([horizontal, horizontal], axis=3)
    shifted = lax.dynamic_slice_in_dim(doubled, tile_offset[0], extent, 3)
    following = jnp.concatenate([shifted[..., 1:], shifted[..., :1]], axis=3)
    refined_x = jnp.stack([shifted, (shifted + following) * 0.5], axis=4).reshape(
        2, shifted.shape[1], shifted.shape[2], 2 * extent
    )
    arrived = lax.all_to_all(refined_x, "row", split_axis=3, concat_axis=1, tiled=True)
    scalar_ext, x_coarse, y_coarse = (
        extended(scalar, (("row", 2), ("col", 1)), 2),
        extended(arrived[0], (("row", 2), ("col", 1)), 2),
        extended(arrived[1], (("row", 2), ("col", 1)), 2),
    )
    x_refined = refine_rows(x_coarse, 2)[:, 2:-2, 2:-2]
    y_refined = refine_rows(y_coarse, 2)[:, 2:-2, 2:-2]
    halfway = advance(scalar_ext, x_refined, y_refined)
    halfway_ext = extended(halfway, (("row", 2), ("col", 1)), 2)
    scalar_new = advance(halfway_ext, x_refined, y_refined)
    return (velocity_new, scalar_new)


def split(values):
    high = values.astype(jnp.bfloat16)
    return high, (values - high.astype(jnp.float32)).astype(jnp.bfloat16)


def host_split(table):
    table = table.astype(np.float32)
    high = table.astype(jnp.bfloat16)
    return high, (table - high.astype(np.float32)).astype(jnp.bfloat16)


def host_angles(rows, columns, length):
    phases = np.outer(rows, columns) % length
    return phases * (2.0 * np.pi / length)


def y_table(length):
    indices = np.arange(length)
    angles = host_angles(indices, indices, length)
    return host_split(np.concatenate([np.cos(angles), np.sin(angles)], axis=1) / np.sqrt(length))


def x_table(length, block):
    indices = np.arange(length)
    angles = host_angles(indices, indices, length).reshape(length // block, block, length)
    return host_split(
        np.stack([np.cos(angles), -np.sin(angles)], axis=1).reshape(2 * length, length)
        / np.sqrt(length)
    )


def row_weights(lines, height, next_at, last_at):
    weights = np.zeros((height + 8, lines + 8), np.float32)
    place = {**{j: j for j in range(lines)}, lines: next_at, lines + 1: next_at + 1, -1: last_at}
    for fine in range(-2, height + 2):
        base = fine // 2
        row = fine if fine >= 0 else height + 8 + fine
        if fine % 2 == 0:
            weights[row, place[base]] += 1.0
        else:
            weights[row, place[base]] += 0.5
            weights[row, place[base + 1]] += 0.5
    return weights.astype(jnp.bfloat16)


def column_weights(columns, breadth, total):
    weights = np.zeros((columns, total), np.float32)
    for fine in range(-2, breadth + 2):
        base = fine // 2
        at = fine if fine >= 0 else total + fine
        if fine % 2 == 0:
            weights[base + 1, at] += 1.0
        else:
            weights[base + 1, at] += 0.5
            weights[base + 2, at] += 0.5
    return weights.astype(jnp.bfloat16)


def dot(left, right, contract):
    return lax.dot_general(
        left, right, (contract, ((), ())), preferred_element_type=jnp.float32
    )


def dot3(left, right, contract):
    return (
        dot(left[0], right[0], contract)
        + dot(left[0], right[1], contract)
        + dot(left[1], right[0], contract)
    )


def lane_wave(shape, dim, start, length):
    wave = lax.broadcasted_iota(jnp.int32, shape, dim) + start
    return jnp.where(wave < length // 2, wave, wave - length)


def inverse_y(count, block, length, routes, near, spectra, head, tail, table_high, table_low, *rest):
    outs, (spectra_high, spectra_low, lines) = rest[:count], rest[count:]
    col = lax.axis_index("col")
    kappa_y = lane_wave((block, length), 1, 0, length).astype(jnp.float32) / (length // 2)
    kappa_x = lane_wave((block, length), 0, col * block, length).astype(jnp.float32) / (length // 2)
    real = [spectra[f, 0, 0] for f in range(3)]
    imag = [spectra[f, 1, 0] for f in range(3)]
    real.append(-kappa_y * imag[2])
    imag.append(kappa_y * real[2])
    real.append(kappa_y * imag[0] - kappa_x * imag[1])
    imag.append(kappa_x * real[1] - kappa_y * real[0])
    for f in range(5):
        real_pair = split(real[f])
        imag_pair = split(imag[f])
        top = slice(2 * f * block, (2 * f + 1) * block)
        bottom = slice((2 * f + 1) * block, (2 * f + 2) * block)
        for store, re, im in (
            (spectra_high, real_pair[0], imag_pair[0]),
            (spectra_low, real_pair[1], imag_pair[1]),
        ):
            store[top, :length] = re
            store[top, length:] = -im
            store[bottom, :length] = im
            store[bottom, length:] = re
    lines[...] = dot3(
        (table_high[...], table_low[...]), (spectra_high[...], spectra_low[...]), ((1,), (1,))
    )
    wide = 2 * block
    sub = lax.broadcasted_iota(jnp.int32, (8, wide), 0)
    for s in range(count):
        dest = routes[0, s, col]
        base = pl.multiple_of(dest * block, 8)
        for f in range(5):
            outs[s][f * block : (f + 1) * block, :] = lines[
                pl.ds(base, block), f * wide : (f + 1) * wide
            ]
        following = pl.multiple_of(lax.rem(dest + 1, count) * block, 8)
        before = pl.multiple_of(lax.rem(dest + count - 1, count) * block + block - 8, 8)
        next_x = lines[pl.ds(following, 8), 0:wide]
        next_y = pltpu.roll(lines[pl.ds(following, 8), wide : 2 * wide], 2, 0)
        last_x = lines[pl.ds(before, 8), 0:wide]
        last_y = pltpu.roll(lines[pl.ds(before, 8), wide : 2 * wide], 7, 0)
        rim = jnp.where(sub < 2, next_x, jnp.where(sub < 4, next_y, jnp.where(sub < 7, last_y, last_x)))
        at = 5 * block
        outs[s][at : at + 8, :] = rim
        at += 8
        edges = ([tail] if s == near[0] else []) + ([head] if s == near[1] else [])
        for edge in edges:
            for p in range(edge.shape[0]):
                for b in range(edge.shape[2] // wide):
                    outs[s][at : at + 8, :] = edge[p, :, b * wide : (b + 1) * wide]
                    at += 8


def middle(count, rows, block, length, planes, breadth, near, offsets, arrivals, departures, *refs):
    slabs = refs[:count]
    first, final, table_high, table_low = refs[count : count + 4]
    outs = refs[count + 4 : 2 * count + 4]
    windows = refs[2 * count + 4 : 2 * count + 4 + rows]
    rim_out, lhs_high, lhs_low, freq = refs[2 * count + 4 + rows :]
    col, row, offset = lax.axis_index("col"), lax.axis_index("row"), offsets[0]
    wide = 2 * block
    lane = lax.broadcasted_iota(jnp.int32, (1, wide), 1)
    for s in range(count):
        source = arrivals[1, s, col]
        at = pl.multiple_of(source * wide, wide)
        value = slabs[s][0 : 5 * block, :]
        high, low = split(value)
        lhs_high[0 : 5 * block, pl.ds(at, wide)] = high
        lhs_low[0 : 5 * block, pl.ds(at, wide)] = low
        wave = lax.rem(lane, block) + source * block
        wave = jnp.where(wave < length // 2, wave, wave - length)
        kappa = wave.astype(jnp.float32) / (length // 2)
        kappa = jnp.where(lane < block, kappa, -kappa)
        spin = jnp.concatenate(
            [
                pltpu.roll(value[2 * block : 3 * block], block, 1) * kappa,
                slabs[s][5 * block : 5 * block + 8, :],
                jnp.zeros((8, wide), jnp.float32),
            ]
        )
        high, low = split(spin)
        lhs_high[5 * block :, pl.ds(at, wide)] = high
        lhs_low[5 * block :, pl.ds(at, wide)] = low
    table = (table_high[...], table_low[...])
    physical = dot3((lhs_high[...], lhs_low[...]), table, ((1,), (0,)))
    u, v, w, spin_x, spin_z, spin_y = [physical[f * block : (f + 1) * block] for f in range(6)]
    product = jnp.concatenate([v * spin_z - w * spin_y, w * spin_x - u * spin_z, u * spin_y - v * spin_x])
    freq[...] = dot3(split(product), table, ((1,), (1,)))
    for s in range(count):
        at = pl.multiple_of(departures[0, s, col] * wide, wide)
        outs[s][...] = freq[:, pl.ds(at, wide)]
    rim = physical[6 * block : 6 * block + 8]
    sub = lax.broadcasted_iota(jnp.int32, (8, wide), 0)
    pieces = breadth // wide
    edge = 5 * block + 8
    for p in range(planes):
        for b in range(pieces):
            step = 8 * (p * pieces + b)
            upper = slabs[near[0]][edge + step : edge + step + 8, :]
            lower = slabs[near[1]][edge + step : edge + step + 8, :]
            rim_out[p, :, b * wide : (b + 1) * wide] = jnp.where(sub < 4, lower, upper)
    cells = breadth // 2
    height = first.shape[1]
    kept = windows[0].shape[0] - planes * (height + 8)
    lines = block + 8
    span = kept // (2 * lines)
    for s in range(rows):
        target = lax.rem(row + s, rows)
        shift = lax.rem(2 * length + 1 - offset - target * cells, length)
        for f, field in enumerate((u, v)):
            rolled = pltpu.roll(jnp.concatenate([field, rim]), shift, 1)
            for b in range(span):
                at = (f * span + b) * lines
                windows[s][at : at + lines, :] = rolled[:, b * wide : (b + 1) * wide]
        if s > 0:
            for p in range(planes):
                at = kept + p * (height + 8)
                windows[s][at : at + height, :] = jnp.where(lane < block, first[p], final[p])
                windows[s][at + height : at + height + 8, :] = jnp.where(
                    lane < block, rim_out[p, :, 0:wide], rim_out[p, :, breadth - wide : breadth]
                )


def transport(rows, block, planes, *refs):
    scalar, rim = refs[0], refs[1]
    windows = refs[2 : 2 + rows]
    weights_x, weights_y, across, out = refs[2 + rows :]
    row = lax.axis_index("row")
    wide = 2 * block
    height, breadth = scalar.shape[1], scalar.shape[2]
    lines = block + 8
    kept = windows[0].shape[0] - planes * (height + 8)
    span = kept // (2 * lines)
    lane = lax.broadcasted_iota(jnp.int32, (1, wide), 1)
    per_row = planes // rows
    tall = height + 8

    def shifted(values, amount, axis):
        return pltpu.roll(values, (-amount) % values.shape[axis], axis)

    for s in range(rows):
        source = lax.rem(row + rows - s, rows)
        speeds = []
        for f, weights in enumerate((weights_x, weights_y)):
            coarse = jnp.concatenate(
                [windows[s][(f * span + b) * lines : (f * span + b + 1) * lines, :] for b in range(span)],
                axis=1,
            )
            high, low = split(coarse)
            taller = dot(weights[...], high, ((1,), (0,))) + dot(weights[...], low, ((1,), (0,)))
            high, low = split(taller)
            speeds.append(dot(high, across[...], ((1,), (0,))) + dot(low, across[...], ((1,), (0,))))
        x_speed, y_speed = speeds
        for q in range(per_row):
            p = source * per_row + q
            sides = []
            for part in (1 % rows, rows - 1):
                sides.append(windows[part][pl.ds(pl.multiple_of(kept + p * tall, 8), tall), :])
            values = jnp.concatenate(
                [
                    jnp.concatenate([scalar[p], rim[p]], axis=0),
                    jnp.where(lane < block, sides[1], sides[0]),
                ],
                axis=1,
            )
            for _ in range(2):
                right, left = shifted(values, 1, 1), shifted(values, -1, 1)
                right2, left2 = shifted(values, 2, 1), shifted(values, -2, 1)
                below, above = shifted(values, 1, 0), shifted(values, -1, 0)
                below2, above2 = shifted(values, 2, 0), shifted(values, -2, 0)
                grad_x = left2 - right2 + 8.0 * (right - left)
                grad_y = above2 - below2 + 8.0 * (below - above)
                near = (right + left) + (below + above)
                far = (right2 + left2) + (below2 + above2)
                spread = 16.0 * near - far - 60.0 * values
                values = values + (substep / 12.0) * (
                    diffusivity * spread - (x_speed * grad_x + y_speed * grad_y)
                )
            out[p] = values[:height, :breadth]


def forward_y(count, block, length, departures, *refs):
    slabs = refs[:count]
    spectra, table_high, table_low, out, gathered = refs[count:]
    col = lax.axis_index("col")
    wide = 2 * block
    for s in range(count):
        source = departures[1, s, col]
        at = pl.multiple_of(source * block, 8)
        for f in range(3):
            gathered[pl.ds(at, block), f * wide : (f + 1) * wide] = slabs[s][
                f * block : (f + 1) * block, :
            ]
    parts = dot3(split(gathered[...].T), (table_high[...], table_low[...]), ((1,), (0,)))
    wave_y = lane_wave((block, length), 1, 0, length)
    wave_x = lane_wave((block, length), 0, col * block, length)
    kappa_y = wave_y.astype(jnp.float32) / (length // 2)
    kappa_x = wave_x.astype(jnp.float32) / (length // 2)
    damping = jnp.exp(-viscosity * time_step * (kappa_x * kappa_x + kappa_y * kappa_y))
    retained = (3 * jnp.abs(wave_x) < length) & (3 * jnp.abs(wave_y) < length)
    for f in range(3):
        real = parts[f * wide : f * wide + block]
        imag = parts[f * wide + block : (f + 1) * wide]
        forcing_real = real[:, :length] + imag[:, length:]
        forcing_imag = imag[:, :length] - real[:, length:]
        out[f, 0, 0] = damping * (
            spectra[f, 0, 0] + time_step * jnp.where(retained, forcing_real, 0.0)
        )
        out[f, 1, 0] = damping * (
            spectra[f, 1, 0] + time_step * jnp.where(retained, forcing_imag, 0.0)
        )


def whole_spec(shape):
    return pl.BlockSpec(shape, lambda *_: (0,) * len(shape))


def kernel_call(body, scalars, operands, specs, out_shapes, scratch=(), cost=None):
    return pl.pallas_call(
        body,
        grid=(1,),
        in_specs=[pl.BlockSpec(memory_space=pltpu.SMEM)] * len(scalars) + specs,
        out_specs=[whole_spec(s) for s in out_shapes],
        out_shape=[jax.ShapeDtypeStruct(s, jnp.float32) for s in out_shapes],
        scratch_shapes=list(scratch),
        compiler_params=pltpu.CompilerParams(vmem_limit_bytes=20 * 1024 * 1024),
        cost_estimate=cost,
    )(*scalars, *operands)


def shift_routes(count):
    order = sorted(range(1, count), key=lambda s: (-min(s, count - s), s))
    return [tuple((i + s) % count for i in range(count)) for s in order]


def needed_routes(count, needed):
    pairs = [[int(needed[d] and i != d) for d in range(count)] for i in range(count)]
    spare = [i for i in range(count) for _ in range(count - 1 - sum(pairs[i]))]
    idle = [d for d in range(count) if not needed[d] for _ in range(count - 1)]
    for i, d in zip(spare, idle):
        pairs[i][d] += 1
    far = [[2 * abs(i - d) if needed[d] else 0 for d in range(count)] for i in range(count)]
    routes = []
    for _ in range(count - 1):
        best = max(
            (
                p
                for p in itertools.permutations(range(count))
                if all(pairs[i][p[i]] for i in range(count))
            ),
            key=lambda p: sum(far[i][p[i]] for i in range(count)),
        )
        for i, d in enumerate(best):
            pairs[i][d] -= 1
        routes.append(best)
    return routes


def route_table(routes):
    count = len(routes[0])
    targets = [list(range(count))] + [list(r) for r in routes]
    sources = [[t.index(i) for i in range(count)] for t in targets]
    return jnp.asarray(np.array([targets, sources], np.int32))


def exchange(slabs, axis, routes):
    return [slabs[0]] + [
        lax.ppermute(slab, axis, list(enumerate(route))) for slab, route in zip(slabs[1:], routes)
    ]


def fast_device(velocity_hat, scalar, tile_offset):
    return fast_step(velocity_hat, scalar, tile_offset)


def fast_step(velocity_hat, scalar, tile_offset):
    length = velocity_hat.shape[4]
    block = velocity_hat.shape[3]
    planes, height, breadth = scalar.shape
    count = lax.axis_size("col")
    rows = lax.axis_size("row")
    wide = 2 * block
    arrival_routes = shift_routes(count)
    wave = np.arange(length)
    wave = np.where(wave < length // 2, wave, wave - length)
    kept = (3 * np.abs(wave) < length).reshape(count, block).any(axis=1)
    departure_routes = needed_routes(count, kept.tolist())
    near = [1 + [r[0] for r in arrival_routes].index(s) for s in (1, count - 1)]
    arrivals, departures = route_table(arrival_routes), route_table(departure_routes)
    y_high, y_low = [jnp.asarray(t) for t in y_table(length)]
    x_high, x_low = [jnp.asarray(t) for t in x_table(length, block)]
    y_specs = [whole_spec(y_high.shape)] * 2
    x_specs = [whole_spec(x_high.shape)] * 2
    edge_rows = 8 * planes * (breadth // wide)
    slab_rows = [
        5 * block + 8 + edge_rows * (s in near) for s in range(count)
    ]
    slabs = kernel_call(
        lambda routes, *refs: inverse_y(count, block, length, routes, near, *refs),
        [arrivals],
        [velocity_hat, scalar, scalar, y_high, y_low],
        [
            whole_spec(velocity_hat.shape),
            pl.BlockSpec((planes, 8, breadth), lambda *_: (0, 0, 0)),
            pl.BlockSpec((planes, 8, breadth), lambda *_: (0, height // 8 - 1, 0)),
        ]
        + y_specs,
        [(r, wide) for r in slab_rows],
        [
            pltpu.VMEM((10 * block, 2 * length), jnp.bfloat16),
            pltpu.VMEM((10 * block, 2 * length), jnp.bfloat16),
            pltpu.VMEM((length, 10 * block), jnp.float32),
        ],
    )
    slabs = exchange(slabs, "col", arrival_routes)
    lines = block + 8
    columns = -(-(breadth // 2 + 3) // wide) * wide
    window_rows = 2 * lines * (columns // wide) + planes * (height + 8)
    results = kernel_call(
        functools.partial(middle, count, rows, block, length, planes, breadth, near),
        [tile_offset, arrivals, departures],
        [*slabs, scalar, scalar, x_high, x_low],
        [whole_spec(s.shape) for s in slabs]
        + [
            pl.BlockSpec((planes, height, wide), lambda *_: (0, 0, 0)),
            pl.BlockSpec((planes, height, wide), lambda *_: (0, 0, breadth // wide - 1)),
        ]
        + x_specs,
        [(3 * block, wide)] * count + [(window_rows, wide)] * rows + [(planes, 8, breadth)],
        [
            pltpu.VMEM((6 * block + 16, 2 * length), jnp.bfloat16),
            pltpu.VMEM((6 * block + 16, 2 * length), jnp.bfloat16),
            pltpu.VMEM((3 * block, 2 * length), jnp.float32),
        ],
    )
    windows = exchange(results[count : count + rows], "row", [
        tuple((i + s) % rows for i in range(rows)) for s in range(1, rows)
    ])
    returned = exchange(results[:count], "col", departure_routes)
    rim = results[count + rows]
    weights = [
        jnp.asarray(row_weights(block, height, block, block + 7)),
        jnp.asarray(row_weights(block, height, block + 2, block + 6)),
        jnp.asarray(column_weights(columns, breadth, breadth + wide)),
    ]
    (scalar_new,) = kernel_call(
        functools.partial(transport, rows, block, planes),
        [],
        [scalar, rim, *windows, *weights],
        [whole_spec(x.shape) for x in (scalar, rim, *windows, *weights)],
        [scalar.shape],
        cost=pl.CostEstimate(flops=4_000_000_000, bytes_accessed=0, transcendentals=0),
    )
    (velocity_new,) = kernel_call(
        functools.partial(forward_y, count, block, length),
        [departures],
        [*returned, velocity_hat, y_high, y_low],
        [whole_spec(x.shape) for x in (*returned, velocity_hat)] + y_specs,
        [velocity_hat.shape],
        [pltpu.VMEM((length, 3 * wide), jnp.float32)],
    )
    return velocity_new, scalar_new


def fits(mesh, velocity_hat, scalar):
    count, rows = mesh.shape["col"], mesh.shape["row"]
    planes = velocity_hat.shape[2] // (mesh.shape["group"] * rows)
    length = velocity_hat.shape[4]
    block = velocity_hat.shape[3] // count
    height, breadth = scalar.shape[1] // count, scalar.shape[2] // rows
    return (
        planes == 1
        and 2 < count <= 8
        and 1 < rows <= 8
        and (2 * block) % 128 == 0
        and height == 2 * block
        and breadth * rows == 2 * length
        and breadth % (2 * block) == 0
        and breadth // 2 + 3 <= length
    )


def solution(mesh):

    def step(velocity_hat, scalar, tile_offset):
        fast = fits(mesh, velocity_hat, scalar)
        mapped = jax.shard_map(
            fast_device if fast else per_device,
            mesh=mesh,
            in_specs=(P(None, None, ("group", "row"), "col", None), P("group", "col", "row"), P()),
            out_specs=(P(None, None, ("group", "row"), "col", None), P("group", "col", "row")),
            check_vma=False,
        )
        return mapped(velocity_hat, scalar, tile_offset)

    return step
```

profile of v0, /device:TPU:0, one launch (start us, length us, event | category | flops | bytes accessed | tf_op | source)
XLA Modules:
  0.0 78.3 jit_solution(230208994358730979)
XLA Ops:
  0.6 0.0 copy-start.11
  0.6 0.7 copy-done.11
  1.3 1.0 %copy-done = f32[2,128,512]{2,1,0:T(8,128)S(1)} copy-done((f32[2,128,512]{2,1,0:T(8,128)S(1)}, f32[2,128,512]{2,1,0:T(8,128)}, u32[]{:S(2)}) %copy-start) | copy-done | bytes 524312
  2.4 1.2 %copy-done.2 = bf16[512,1024]{1,0:T(8,128)(2,1)S(1)} copy-done((bf16[512,1024]{1,0:T(8,128)(2,1)S(1)}, bf16[512,1024]{1,0:T(8,128)(2,1)}, u32[]{:S(2)}) %copy-start.2) | copy-done | bytes 1048600
  3.6 1.2 %copy-done.4 = bf16[512,1024]{1,0:T(8,128)(2,1)S(1)} copy-done((bf16[512,1024]{1,0:T(8,128)(2,1)S(1)}, bf16[512,1024]{1,0:T(8,128)(2,1)}, u32[]{:S(2)}) %copy-start.4) | copy-done | bytes 1048600
  4.8 1.1 %copy-done.6 = f32[3,2,1,64,512]{4,3,2,1,0:T(8,128)S(1)} copy-done((f32[3,2,1,64,512]{4,3,2,1,0:T(8,128)S(1)}, f32[3,2,1,64,512]{4,3,2,1,0:T(8,128)}, u32[]{:S(2)}) %copy-start.6) | copy-done | bytes 786456
  6.0 3.4 %shard_map.131 = (f32[328,128]{1,0:T(8,128)S(1)}, f32[328,128]{1,0:T(8,128)S(1)}, f32[328,128]{1,0:T(8,128)S(1)}, f32[328,128]{1,0:T(8,128)S(1)}, f32[328,128]{1...) custom-call(s32[2,8,8]{2,1,0:T(8,128)S(1)} %copy-done.11, ...), custom_call_target="tpu_custom_call" | custom-call | tf_op jit(solution)/shard_map/pallas_call | solution.py:466
  9.4 0.0 copy-start.10
  9.4 4.1 %collective-permute-start = (f32[328,128]{1,0:T(8,128)S(1)}, f32[328,128]{1,0:T(8,128)S(1)}, u32[]{:S(2)}, u32[]{:S(2)}) collective-permute-start(f32[328,128]{1,0:T(8,128)S(1)} %get-tuple-element.22), channel_id=1, source_target_pairs={{0,4},{1,5},{2,6},{3,7},{4,0},{5,1},{6,2},{7,3},{8,12},{9,13},{10,... | collective-permute-start | bytes 503816 | tf_op jit(solution)/shard_map/ppermute | solution.py:515
  13.5 2.5 %collective-permute-start.1 = (f32[328,128]{1,0:T(8,128)S(1)}, f32[328,128]{1,0:T(8,128)S(1)}, u32[]{:S(2)}, u32[]{:S(2)}) collective-permute-start(f32[328,128]{1,0:T(8,128)S(1)} %get-tuple-element.23), channel_id=1, source_target_pairs={{0,3},{1,4},{2,5},{3,6},{4,7},{5,0},{6,1},{7,2},{8,11},{9,12},{10,... | collective-permute-start | bytes 503816 | tf_op jit(solution)/shard_map/ppermute | solution.py:515
  16.1 0.0 collective-permute-start.5
  16.1 4.7 %collective-permute-start.6 = (f32[392,128]{1,0:T(8,128)S(1)}, f32[392,128]{1,0:T(8,128)S(1)}, u32[]{:S(2)}, u32[]{:S(2)}) collective-permute-start(f32[392,128]{1,0:T(8,128)S(1)} %get-tuple-element.28), channel_id=1, source_target_pairs={{0,7},{1,0},{2,1},{3,2},{4,3},{5,4},{6,5},{7,6},{8,15},{9,8},{10,9... | collective-permute-start | bytes 602120 | tf_op jit(solution)/shard_map/ppermute | solution.py:515
  20.8 0.0 collective-permute-start.2
  20.8 5.1 %collective-permute-done.refs_1_ = f32[328,128]{1,0:T(8,128)S(1)} collective-permute-done((f32[328,128]{1,0:T(8,128)S(1)}, f32[328,128]{1,0:T(8,128)S(1)}, u32[]{:S(2)}, u32[]{:S(2)}) %collective-permute-start) | collective-permute-done | bytes 167968 | tf_op jit(solution)/shard_map/ppermute | solution.py:515
  25.9 0.0 collective-permute-start.3
  25.9 11.0 %collective-permute-done.1.refs_2_ = f32[328,128]{1,0:T(8,128)S(1)} collective-permute-done((f32[328,128]{1,0:T(8,128)S(1)}, f32[328,128]{1,0:T(8,128)S(1)}, u32[]{:S(2)}, u32[]{:S(2)}) %collective-permute-start.1) | collective-permute-done | bytes 167968 | tf_op jit(solution)/shard_map/ppermute | solution.py:515
  36.9 0.0 collective-permute-start.4
  37.5 3.7 %collective-permute-done.2.refs_3_ = f32[328,128]{1,0:T(8,128)S(1)} collective-permute-done((f32[328,128]{1,0:T(8,128)S(1)}, f32[328,128]{1,0:T(8,128)S(1)}, u32[]{:S(2)}, u32[]{:S(2)}) %collective-permute-start.2) | collective-permute-done | bytes 167968 | tf_op jit(solution)/shard_map/ppermute | solution.py:515
  41.2 0.0 collective-permute-done.3.refs_4_
  41.2 1.5 %collective-permute-done.4.refs_5_ = f32[328,128]{1,0:T(8,128)S(1)} collective-permute-done((f32[328,128]{1,0:T(8,128)S(1)}, f32[328,128]{1,0:T(8,128)S(1)}, u32[]{:S(2)}, u32[]{:S(2)}) %collective-permute-start.4) | collective-permute-done | bytes 167968 | tf_op jit(solution)/shard_map/ppermute | solution.py:515
  42.8 0.0 collective-permute-done.5.refs_6_
  42.8 0.0 collective-permute-done.6.refs_7_
  42.8 0.0 copy-start.3
  42.8 0.0 copy-start.5
  42.8 0.0 copy-start.7
  42.8 3.9 %shard_map.132 = (f32[192,128]{1,0:T(8,128)S(1)}, f32[192,128]{1,0:T(8,128)S(1)}, f32[192,128]{1,0:T(8,128)S(1)}, f32[192,128]{1,0:T(8,128)S(1)}, f32[192,128]{1...) custom-call(s32[1]{0:T(128)S(6)} %copy.14.offsets, ...), custom_call_target="tpu_custom_call" | custom-call | tf_op jit(solution)/shard_map/pallas_call | solution.py:466
  46.8 1.5 %collective-permute-start.14 = (f32[704,128]{1,0:T(8,128)S(1)}, f32[704,128]{1,0:T(8,128)S(1)}, u32[]{:S(2)}, u32[]{:S(2)}) collective-permute-start(f32[704,128]{1,0:T(8,128)S(1)} %get-tuple-element.39), channel_id=1, source_target_pairs={{0,8},{8,0},{1,9},{9,1},{2,10},{10,2},{3,11},{11,3},{4,12},{12,4},... | collective-permute-start | bytes 1081352 | tf_op jit(solution)/shard_map/ppermute | solution.py:515
  48.2 6.5 %collective-permute-start.7 = (f32[192,128]{1,0:T(8,128)S(1)}, f32[192,128]{1,0:T(8,128)S(1)}, u32[]{:S(2)}, u32[]{:S(2)}) collective-permute-start(f32[192,128]{1,0:T(8,128)S(1)} %get-tuple-element.30), channel_id=1, source_target_pairs={{0,5},{1,6},{2,7},{3,3},{4,4},{5,0},{6,1},{7,2},{8,13},{9,14},{10,... | collective-permute-start | bytes 294920 | tf_op jit(solution)/shard_map/ppermute | solution.py:515
  54.8 0.4 collective-permute-start.8
  55.2 1.9 %collective-permute-start.9 = (f32[192,128]{1,0:T(8,128)S(1)}, f32[192,128]{1,0:T(8,128)S(1)}, u32[]{:S(2)}, u32[]{:S(2)}) collective-permute-start(f32[192,128]{1,0:T(8,128)S(1)} %get-tuple-element.32), channel_id=1, source_target_pairs={{0,7},{1,3},{2,5},{3,6},{4,1},{5,2},{6,4},{7,0},{8,15},{9,11},{10,... | collective-permute-start | bytes 294920 | tf_op jit(solution)/shard_map/ppermute | solution.py:515
  57.1 0.0 collective-permute-start.10
  57.1 7.0 %collective-permute-done.7.refs_1_ = f32[192,128]{1,0:T(8,128)S(1)} collective-permute-done((f32[192,128]{1,0:T(8,128)S(1)}, f32[192,128]{1,0:T(8,128)S(1)}, u32[]{:S(2)}, u32[]{:S(2)}) %collective-permute-start.7) | collective-permute-done | bytes 98336 | tf_op jit(solution)/shard_map/ppermute | solution.py:515
  64.1 0.0 collective-permute-start.11
  64.1 0.0 collective-permute-done.8.refs_2_
  64.1 0.0 collective-permute-start.12
  64.1 0.0 collective-permute-done.9.refs_3_
  64.1 2.9 %collective-permute-start.13 = (f32[192,128]{1,0:T(8,128)S(1)}, f32[192,128]{1,0:T(8,128)S(1)}, u32[]{:S(2)}, u32[]{:S(2)}) collective-permute-start(f32[192,128]{1,0:T(8,128)S(1)} %get-tuple-element.36), channel_id=1, source_target_pairs={{0,3},{1,0},{2,1},{3,2},{4,5},{5,6},{6,7},{7,4},{8,11},{9,8},{10,9... | collective-permute-start | bytes 294920 | tf_op jit(solution)/shard_map/ppermute | solution.py:515
  67.0 0.0 collective-permute-done.10.refs_4_
  67.0 1.7 %collective-permute-done.11.refs_5_ = f32[192,128]{1,0:T(8,128)S(1)} collective-permute-done((f32[192,128]{1,0:T(8,128)S(1)}, f32[192,128]{1,0:T(8,128)S(1)}, u32[]{:S(2)}, u32[]{:S(2)}) %collective-permute-start.11) | collective-permute-done | bytes 98336 | tf_op jit(solution)/shard_map/ppermute | solution.py:515
  68.7 1.6 %collective-permute-done.12.refs_6_ = f32[192,128]{1,0:T(8,128)S(1)} collective-permute-done((f32[192,128]{1,0:T(8,128)S(1)}, f32[192,128]{1,0:T(8,128)S(1)}, u32[]{:S(2)}, u32[]{:S(2)}) %collective-permute-start.12) | collective-permute-done | bytes 98336 | tf_op jit(solution)/shard_map/ppermute | solution.py:515
  70.2 1.4 %collective-permute-done.13.refs_7_ = f32[192,128]{1,0:T(8,128)S(1)} collective-permute-done((f32[192,128]{1,0:T(8,128)S(1)}, f32[192,128]{1,0:T(8,128)S(1)}, u32[]{:S(2)}, u32[]{:S(2)}) %collective-permute-start.13) | collective-permute-done | bytes 98336 | tf_op jit(solution)/shard_map/ppermute | solution.py:515
  71.7 0.0 copy-done.3
  71.7 0.0 copy-start.12
  71.7 0.0 copy-start.13
  71.7 0.0 copy-start.14
  71.7 3.1 %shard_map.133 = f32[3,2,1,64,512]{4,3,2,1,0:T(8,128)} custom-call(s32[2,8,8]{2,1,0:T(8,128)S(1)} %copy-done.10, f32[192,128]{1,0:T(8,128)S(1)} %get-tuple-element.29.refs_0_, f32[192,128]{1,0:T(8,128)S(1)} %collective-permute-done.7.refs_1_, f32[192,128]{1,0:T(8,128)S(1)} %collective-permute-done.8.refs_2_, f32[192,128]{1,0:T(8,128)S(1)} %collective-permute-done.9.refs_3_, ...), custom_call_target="tpu_custom_call" | custom-call | tf_op jit(solution)/shard_map/pallas_call | solution.py:466
  74.8 0.0 collective-permute-done.14.refs_3_
  74.8 3.5 %shard_map.134 = f32[2,128,512]{2,1,0:T(8,128)} custom-call(f32[2,128,512]{2,1,0:T(8,128)S(1)} %copy-done.1, f32[2,8,512]{2,1,0:T(8,128)S(1)} %get-tuple-element.37.refs_1_, f32[704,128]{1,0:T(8,128)S(1)} %get-tuple-element.38.refs_2_, f32[704,128]{1,0:T(8,128)S(1)} %collective-permute-done.14.refs_3_, bf16[136,72]{1,0:T(8,128)(2,1)S(1)} %copy-done.14, ...), custom_call_target="tpu_custom_call" | custom-call | flops 4000000000 | tf_op jit(solution)/shard_map/pallas_call | solution.py:466
  (16 shorter events, 0.0 us)
Async XLA Ops:
  0.6 0.7 copy-start.11
  1.3 1.0 %copy-start = (f32[2,128,512]{2,1,0:T(8,128)S(1)}, f32[2,128,512]{2,1,0:T(8,128)}, u32[]{:S(2)}) copy-start(f32[2,128,512]{2,1,0:T(8,128)} %refs_0_.3) | copy-start | bytes 1572868
  2.4 1.2 %copy-start.2 = (bf16[512,1024]{1,0:T(8,128)(2,1)S(1)}, bf16[512,1024]{1,0:T(8,128)(2,1)}, u32[]{:S(2)}) copy-start(bf16[512,1024]{1,0:T(8,128)(2,1)} %constant.21.clone.refs_4_.refs_10_) | copy-start | bytes 3145732
  3.6 1.2 %copy-start.4 = (bf16[512,1024]{1,0:T(8,128)(2,1)S(1)}, bf16[512,1024]{1,0:T(8,128)(2,1)}, u32[]{:S(2)}) copy-start(bf16[512,1024]{1,0:T(8,128)(2,1)} %constant.20.clone.refs_3_.refs_9_) | copy-start | bytes 3145732
  4.8 1.1 %copy-start.6 = (f32[3,2,1,64,512]{4,3,2,1,0:T(8,128)S(1)}, f32[3,2,1,64,512]{4,3,2,1,0:T(8,128)}, u32[]{:S(2)}) copy-start(f32[3,2,1,64,512]{4,3,2,1,0:T(8,128)} %refs_8_.3) | copy-start | bytes 2359300
  6.0 36.8 %copy-start.1 = (f32[2,128,512]{2,1,0:T(8,128)S(1)}, f32[2,128,512]{2,1,0:T(8,128)}, u32[]{:S(2)}) copy-start(f32[2,128,512]{2,1,0:T(8,128)} %refs_0_.3) | copy-start | bytes 1572868
  6.0 36.8 %copy-start.8 = (bf16[1024,512]{1,0:T(8,128)(2,1)S(1)}, bf16[1024,512]{1,0:T(8,128)(2,1)}, u32[]{:S(2)}) copy-start(bf16[1024,512]{1,0:T(8,128)(2,1)} %constant.23.clone.refs_11_) | copy-start | bytes 3145732
  6.0 36.8 %copy-start.9 = (bf16[1024,512]{1,0:T(8,128)(2,1)S(1)}, bf16[1024,512]{1,0:T(8,128)(2,1)}, u32[]{:S(2)}) copy-start(bf16[1024,512]{1,0:T(8,128)(2,1)} %constant.22.clone.refs_10_) | copy-start | bytes 3145732
  9.4 33.4 %copy-start.10 = (s32[2,8,8]{2,1,0:T(8,128)S(1)}, s32[2,8,8]{2,1,0:T(8,128)}, u32[]{:S(2)}) copy-start(s32[2,8,8]{2,1,0:T(8,128)} %constant.19.clone.departures) | copy-start | bytes 1540
  9.4 16.5 %collective-permute-start = (f32[328,128]{1,0:T(8,128)S(1)}, f32[328,128]{1,0:T(8,128)S(1)}, u32[]{:S(2)}, u32[]{:S(2)}) collective-permute-start(f32[328,128]{1,0:T(8,128)S(1)} %get-tuple-element.22), channel_id=1, source_target_pairs={{0,4},{1,5},{2,6},{3,7},{4,0},{5,1},{6,2},{7,3},{8,12},{9,13},{10,... | collective-permute-start | bytes 503816 | tf_op jit(solution)/shard_map/ppermute | solution.py:515
  13.5 23.3 %collective-permute-start.1 = (f32[328,128]{1,0:T(8,128)S(1)}, f32[328,128]{1,0:T(8,128)S(1)}, u32[]{:S(2)}, u32[]{:S(2)}) collective-permute-start(f32[328,128]{1,0:T(8,128)S(1)} %get-tuple-element.23), channel_id=1, source_target_pairs={{0,3},{1,4},{2,5},{3,6},{4,7},{5,0},{6,1},{7,2},{8,11},{9,12},{10,... | collective-permute-start | bytes 503816 | tf_op jit(solution)/shard_map/ppermute | solution.py:515
  16.1 26.7 %collective-permute-start.5 = (f32[392,128]{1,0:T(8,128)S(1)}, f32[392,128]{1,0:T(8,128)S(1)}, u32[]{:S(2)}, u32[]{:S(2)}) collective-permute-start(f32[392,128]{1,0:T(8,128)S(1)} %get-tuple-element.27), channel_id=1, source_target_pairs={{0,1},{1,2},{2,3},{3,4},{4,5},{5,6},{6,7},{7,0},{8,9},{9,10},{10,1... | collective-permute-start | bytes 602120 | tf_op jit(solution)/shard_map/ppermute | solution.py:515
  16.1 26.7 %collective-permute-start.6 = (f32[392,128]{1,0:T(8,128)S(1)}, f32[392,128]{1,0:T(8,128)S(1)}, u32[]{:S(2)}, u32[]{:S(2)}) collective-permute-start(f32[392,128]{1,0:T(8,128)S(1)} %get-tuple-element.28), channel_id=1, source_target_pairs={{0,7},{1,0},{2,1},{3,2},{4,3},{5,4},{6,5},{7,6},{8,15},{9,8},{10,9... | collective-permute-start | bytes 602120 | tf_op jit(solution)/shard_map/ppermute | solution.py:515
  20.8 20.4 %collective-permute-start.2 = (f32[328,128]{1,0:T(8,128)S(1)}, f32[328,128]{1,0:T(8,128)S(1)}, u32[]{:S(2)}, u32[]{:S(2)}) collective-permute-start(f32[328,128]{1,0:T(8,128)S(1)} %get-tuple-element.24), channel_id=1, source_target_pairs={{0,5},{1,6},{2,7},{3,0},{4,1},{5,2},{6,3},{7,4},{8,13},{9,14},{10,... | collective-permute-start | bytes 503816 | tf_op jit(solution)/shard_map/ppermute | solution.py:515
  25.9 15.3 %collective-permute-start.3 = (f32[328,128]{1,0:T(8,128)S(1)}, f32[328,128]{1,0:T(8,128)S(1)}, u32[]{:S(2)}, u32[]{:S(2)}) collective-permute-start(f32[328,128]{1,0:T(8,128)S(1)} %get-tuple-element.25), channel_id=1, source_target_pairs={{0,2},{1,3},{2,4},{3,5},{4,6},{5,7},{6,0},{7,1},{8,10},{9,11},{10,... | collective-permute-start | bytes 503816 | tf_op jit(solution)/shard_map/ppermute | solution.py:515
  36.9 5.9 %collective-permute-start.4 = (f32[328,128]{1,0:T(8,128)S(1)}, f32[328,128]{1,0:T(8,128)S(1)}, u32[]{:S(2)}, u32[]{:S(2)}) collective-permute-start(f32[328,128]{1,0:T(8,128)S(1)} %get-tuple-element.26), channel_id=1, source_target_pairs={{0,6},{1,7},{2,0},{3,1},{4,2},{5,3},{6,4},{7,5},{8,14},{9,15},{10,... | collective-permute-start | bytes 503816 | tf_op jit(solution)/shard_map/ppermute | solution.py:515
  42.8 28.9 %copy-start.3 = (bf16[512,1024]{1,0:T(8,128)(2,1)S(1)}, bf16[512,1024]{1,0:T(8,128)(2,1)}, u32[]{:S(2)}) copy-start(bf16[512,1024]{1,0:T(8,128)(2,1)} %constant.21.clone.refs_4_.refs_10_) | copy-start | bytes 3145732
  42.8 28.9 %copy-start.5 = (bf16[512,1024]{1,0:T(8,128)(2,1)S(1)}, bf16[512,1024]{1,0:T(8,128)(2,1)}, u32[]{:S(2)}) copy-start(bf16[512,1024]{1,0:T(8,128)(2,1)} %constant.20.clone.refs_3_.refs_9_) | copy-start | bytes 3145732
  42.8 28.8 %copy-start.7 = (f32[3,2,1,64,512]{4,3,2,1,0:T(8,128)S(1)}, f32[3,2,1,64,512]{4,3,2,1,0:T(8,128)}, u32[]{:S(2)}) copy-start(f32[3,2,1,64,512]{4,3,2,1,0:T(8,128)} %refs_8_.3) | copy-start | bytes 2359300
  46.8 28.0 %collective-permute-start.14 = (f32[704,128]{1,0:T(8,128)S(1)}, f32[704,128]{1,0:T(8,128)S(1)}, u32[]{:S(2)}, u32[]{:S(2)}) collective-permute-start(f32[704,128]{1,0:T(8,128)S(1)} %get-tuple-element.39), channel_id=1, source_target_pairs={{0,8},{8,0},{1,9},{9,1},{2,10},{10,2},{3,11},{11,3},{4,12},{12,4},... | collective-permute-start | bytes 1081352 | tf_op jit(solution)/shard_map/ppermute | solution.py:515
  48.2 15.8 %collective-permute-start.7 = (f32[192,128]{1,0:T(8,128)S(1)}, f32[192,128]{1,0:T(8,128)S(1)}, u32[]{:S(2)}, u32[]{:S(2)}) collective-permute-start(f32[192,128]{1,0:T(8,128)S(1)} %get-tuple-element.30), channel_id=1, source_target_pairs={{0,5},{1,6},{2,7},{3,3},{4,4},{5,0},{6,1},{7,2},{8,13},{9,14},{10,... | collective-permute-start | bytes 294920 | tf_op jit(solution)/shard_map/ppermute | solution.py:515
  54.8 9.3 %collective-permute-start.8 = (f32[192,128]{1,0:T(8,128)S(1)}, f32[192,128]{1,0:T(8,128)S(1)}, u32[]{:S(2)}, u32[]{:S(2)}) collective-permute-start(f32[192,128]{1,0:T(8,128)S(1)} %get-tuple-element.31), channel_id=1, source_target_pairs={{0,6},{1,5},{2,3},{3,7},{4,0},{5,4},{6,2},{7,1},{8,14},{9,13},{10,... | collective-permute-start | bytes 294920 | tf_op jit(solution)/shard_map/ppermute | solution.py:515
  55.2 8.9 %collective-permute-start.9 = (f32[192,128]{1,0:T(8,128)S(1)}, f32[192,128]{1,0:T(8,128)S(1)}, u32[]{:S(2)}, u32[]{:S(2)}) collective-permute-start(f32[192,128]{1,0:T(8,128)S(1)} %get-tuple-element.32), channel_id=1, source_target_pairs={{0,7},{1,3},{2,5},{3,6},{4,1},{5,2},{6,4},{7,0},{8,15},{9,11},{10,... | collective-permute-start | bytes 294920 | tf_op jit(solution)/shard_map/ppermute | solution.py:515
  57.1 9.9 %collective-permute-start.10 = (f32[192,128]{1,0:T(8,128)S(1)}, f32[192,128]{1,0:T(8,128)S(1)}, u32[]{:S(2)}, u32[]{:S(2)}) collective-permute-start(f32[192,128]{1,0:T(8,128)S(1)} %get-tuple-element.33), channel_id=1, source_target_pairs={{0,3},{1,7},{2,6},{3,5},{4,2},{5,1},{6,0},{7,4},{8,11},{9,15},{10,... | collective-permute-start | bytes 294920 | tf_op jit(solution)/shard_map/ppermute | solution.py:515
  64.1 4.6 %collective-permute-start.11 = (f32[192,128]{1,0:T(8,128)S(1)}, f32[192,128]{1,0:T(8,128)S(1)}, u32[]{:S(2)}, u32[]{:S(2)}) collective-permute-start(f32[192,128]{1,0:T(8,128)S(1)} %get-tuple-element.34), channel_id=1, source_target_pairs={{0,2},{1,3},{2,0},{3,1},{4,6},{5,7},{6,4},{7,5},{8,10},{9,11},{10,... | collective-permute-start | bytes 294920 | tf_op jit(solution)/shard_map/ppermute | solution.py:515
  64.1 6.2 %collective-permute-start.12 = (f32[192,128]{1,0:T(8,128)S(1)}, f32[192,128]{1,0:T(8,128)S(1)}, u32[]{:S(2)}, u32[]{:S(2)}) collective-permute-start(f32[192,128]{1,0:T(8,128)S(1)} %get-tuple-element.35), channel_id=1, source_target_pairs={{0,1},{1,2},{2,3},{3,0},{4,7},{5,4},{6,5},{7,6},{8,9},{9,10},{10,1... | collective-permute-start | bytes 294920 | tf_op jit(solution)/shard_map/ppermute | solution.py:515
  64.1 7.6 %collective-permute-start.13 = (f32[192,128]{1,0:T(8,128)S(1)}, f32[192,128]{1,0:T(8,128)S(1)}, u32[]{:S(2)}, u32[]{:S(2)}) collective-permute-start(f32[192,128]{1,0:T(8,128)S(1)} %get-tuple-element.36), channel_id=1, source_target_pairs={{0,3},{1,0},{2,1},{3,2},{4,5},{5,6},{6,7},{7,4},{8,11},{9,8},{10,9... | collective-permute-start | bytes 294920 | tf_op jit(solution)/shard_map/ppermute | solution.py:515
  71.7 3.1 %copy-start.12 = (bf16[384,640]{1,0:T(8,128)(2,1)S(1)}, bf16[384,640]{1,0:T(8,128)(2,1)}, u32[]{:S(2)}) copy-start(bf16[384,640]{1,0:T(8,128)(2,1)} %constant.26.clone.refs_6_) | copy-start | bytes 1474564
  71.7 3.1 %copy-start.13 = (bf16[136,72]{1,0:T(8,128)(2,1)S(1)}, bf16[136,72]{1,0:T(8,128)(2,1)}, u32[]{:S(2)}) copy-start(bf16[136,72]{1,0:T(8,128)(2,1)} %constant.25.clone.refs_5_) | copy-start | bytes 58756
  71.7 3.1 %copy-start.14 = (bf16[136,72]{1,0:T(8,128)(2,1)S(1)}, bf16[136,72]{1,0:T(8,128)(2,1)}, u32[]{:S(2)}) copy-start(bf16[136,72]{1,0:T(8,128)(2,1)} %constant.24.clone.refs_4_) | copy-start | bytes 58756
where the time goes:
time: 78.7 us; the launch traced here: 78.3 us
  waiting for transfers between devices  33 us (42%)
  starting transfers between devices  24.6 us (31%)
  Pallas kernels  13.9 us (18%)
  local copies, waits for them, and re-layouts  5.37 us (7%)
  between operations  1.45 us (2%)
    ppermute x15, waiting for transfers between devices, exchange(): lax.ppermute(slab, axis, list(enumerate(route)))  33 us
    ppermute x15, starting transfers between devices, exchange(): lax.ppermute(slab, axis, list(enumerate(route)))  24.6 us
    pallas_call x4, Pallas kernels, kernel_call(): pl.pallas_call(body, grid=(1,), in_specs=[pl.BlockSpec(memory_space=pltpu...  13.9 us
    unnamed x30, local copies, waits for them, and re-layouts  5.37 us
  transfers between devices with their start and end apart: 15, of which 8 were waited for; matrix products, arithmetic and copies ran while one was open for 0% of the time, Pallas kernels for 4%

commit v1 on v0

--- a/solution.py
+++ b/solution.py
@@ -244,9 +244,27 @@
     return jnp.where(wave < length // 2, wave, wave - length)
 
 
-def inverse_y(count, block, length, routes, near, spectra, head, tail, table_high, table_low, *rest):
-    outs, (spectra_high, spectra_low, lines) = rest[:count], rest[count:]
+def inverse_y(count, block, length, shifts, near, spectra_in, scalar_in, high_in, low_in, *rest):
+    outs = rest[:count]
+    spectra, head, tail, table_high, table_low, sems = rest[count : count + 6]
+    spectra_high, spectra_low, lines = rest[count + 6 :]
+    height = scalar_in.shape[1]
+    copies = [
+        pltpu.make_async_copy(source, target, sems.at[n])
+        for n, (source, target) in enumerate(
+            (
+                (spectra_in, spectra),
+                (high_in, table_high),
+                (low_in, table_low),
+                (scalar_in.at[:, 0:8, :], head),
+                (scalar_in.at[:, height - 8 : height, :], tail),
+            )
+        )
+    ]
+    for copy in copies:
+        copy.start()
     col = lax.axis_index("col")
+    copies[0].wait()
     kappa_y = lane_wave((block, length), 1, 0, length).astype(jnp.float32) / (length // 2)
     kappa_x = lane_wave((block, length), 0, col * block, length).astype(jnp.float32) / (length // 2)
     real = [spectra[f, 0, 0] for f in range(3)]
@@ -268,13 +286,17 @@
             store[top, length:] = -im
             store[bottom, :length] = im
             store[bottom, length:] = re
+    copies[1].wait()
+    copies[2].wait()
     lines[...] = dot3(
         (table_high[...], table_low[...]), (spectra_high[...], spectra_low[...]), ((1,), (1,))
     )
+    copies[3].wait()
+    copies[4].wait()
     wide = 2 * block
     sub = lax.broadcasted_iota(jnp.int32, (8, wide), 0)
     for s in range(count):
-        dest = routes[0, s, col]
+        dest = lax.rem(col + shifts[s], count)
         base = pl.multiple_of(dest * block, 8)
         for f in range(5):
             outs[s][f * block : (f + 1) * block, :] = lines[
@@ -511,9 +533,10 @@
 
 
 def exchange(slabs, axis, routes):
-    return [slabs[0]] + [
-        lax.ppermute(slab, axis, list(enumerate(route))) for slab, route in zip(slabs[1:], routes)
-    ]
+    arrived = [slabs[0]]
+    for slab, route in zip(slabs[1:], routes):
+        arrived.append(lax.ppermute(slab, axis, list(enumerate(route))))
+    return arrived
 
 
 def fast_device(velocity_hat, scalar, tile_offset):
@@ -542,18 +565,23 @@
     slab_rows = [
         5 * block + 8 + edge_rows * (s in near) for s in range(count)
     ]
+    hbm = pl.BlockSpec(memory_space=pltpu.HBM)
     slabs = kernel_call(
-        lambda routes, *refs: inverse_y(count, block, length, routes, near, *refs),
-        [arrivals],
-        [velocity_hat, scalar, scalar, y_high, y_low],
+        functools.partial(inverse_y, count, block, length, [0] + [r[0] for r in arrival_routes], near),
+        [],
         [
-            whole_spec(velocity_hat.shape),
-            pl.BlockSpec((planes, 8, breadth), lambda *_: (0, 0, 0)),
-            pl.BlockSpec((planes, 8, breadth), lambda *_: (0, height // 8 - 1, 0)),
-        ]
-        + y_specs,
+            pltpu.with_memory_space_constraint(x, pltpu.HBM)
+            for x in (velocity_hat, scalar, y_high, y_low)
+        ],
+        [hbm] * 4,
         [(r, wide) for r in slab_rows],
         [
+            pltpu.VMEM(velocity_hat.shape, jnp.float32),
+            pltpu.VMEM((planes, 8, breadth), jnp.float32),
+            pltpu.VMEM((planes, 8, breadth), jnp.float32),
+            pltpu.VMEM(y_high.shape, jnp.bfloat16),
+            pltpu.VMEM(y_low.shape, jnp.bfloat16),
+            pltpu.SemaphoreType.DMA((5,)),
             pltpu.VMEM((10 * block, 2 * length), jnp.bfloat16),
             pltpu.VMEM((10 * block, 2 * length), jnp.bfloat16),
             pltpu.VMEM((length, 10 * block), jnp.float32),
@@ -628,7 +656,6 @@
 
 
 def solution(mesh):
-
     def step(velocity_hat, scalar, tile_offset):
         fast = fits(mesh, velocity_hat, scalar)
         mapped = jax.shard_map(

time: 78.7 us -> 74.7 us (0.949)
  local copies, waits for them, and re-layouts: 5.37 us -> 0.07 us
  Pallas kernels: 13.9 us -> 15.3 us
    unnamed x30 -> x22, local copies, waits for them, and re-layouts: 5.37 us -> 0.07 us
    pallas_call x4, Pallas kernels: 13.9 us -> 15.3 us  [kernel_call(): pl.pallas_call(body, grid=(1,), in_specs=[pl.BlockSpec(memory_space=pltpu...]
where the time goes in v1:
time: 74.7 us; the launch traced here: 74.5 us
  waiting for transfers between devices  33 us (44%)
  starting transfers between devices  24.6 us (33%)
  Pallas kernels  15.3 us (20%)
  between operations  1.47 us (2%)
    ppermute x15, waiting for transfers between devices, exchange(): arrived.append(lax.ppermute(slab, axis, list(enumerate(route))))  33 us
    ppermute x15, starting transfers between devices, exchange(): arrived.append(lax.ppermute(slab, axis, list(enumerate(route))))  24.6 us
    pallas_call x4, Pallas kernels, kernel_call(): pl.pallas_call(body, grid=(1,), in_specs=[pl.BlockSpec(memory_space=pltpu...  15.3 us
  transfers between devices with their start and end apart: 15, of which 8 were waited for; matrix products, arithmetic and copies ran while one was open for 0% of the time, Pallas kernels for 4%

profile of v1, /device:TPU:0, one launch (start us, length us, event | category | flops | bytes accessed | tf_op | source)
XLA Modules:
  0.0 74.5 jit_solution(8752656097226181969)
XLA Ops:
  0.6 0.0 copy-start.4
  0.6 0.0 copy-start.5
  0.7 4.7 %shard_map.131 = (f32[328,128]{1,0:T(8,128)S(1)}, f32[328,128]{1,0:T(8,128)S(1)}, f32[328,128]{1,0:T(8,128)S(1)}, f32[328,128]{1,0:T(8,128)S(1)}, f32[328,128]{1...) custom-call(f32[3,2,1,64,512]{4,3,2,1,0:T(8,128)} %refs_8_.3, ...), custom_call_target="tpu_custom_call" | custom-call | tf_op jit(solution)/shard_map/pallas_call | solution.py:488
  5.4 0.0 copy-start.7
  5.4 0.0 copy-start.6
  5.4 4.1 %collective-permute-start = (f32[328,128]{1,0:T(8,128)S(1)}, f32[328,128]{1,0:T(8,128)S(1)}, u32[]{:S(2)}, u32[]{:S(2)}) collective-permute-start(f32[328,128]{1,0:T(8,128)S(1)} %get-tuple-element.22), channel_id=1, source_target_pairs={{0,4},{1,5},{2,6},{3,7},{4,0},{5,1},{6,2},{7,3},{8,12},{9,13},{10,... | collective-permute-start | bytes 503816 | tf_op jit(solution)/shard_map/ppermute | solution.py:538
  9.5 2.5 %collective-permute-start.1 = (f32[328,128]{1,0:T(8,128)S(1)}, f32[328,128]{1,0:T(8,128)S(1)}, u32[]{:S(2)}, u32[]{:S(2)}) collective-permute-start(f32[328,128]{1,0:T(8,128)S(1)} %get-tuple-element.23), channel_id=1, source_target_pairs={{0,3},{1,4},{2,5},{3,6},{4,7},{5,0},{6,1},{7,2},{8,11},{9,12},{10,... | collective-permute-start | bytes 503816 | tf_op jit(solution)/shard_map/ppermute | solution.py:538
  12.1 0.0 collective-permute-start.5
  12.1 4.7 %collective-permute-start.6 = (f32[392,128]{1,0:T(8,128)S(1)}, f32[392,128]{1,0:T(8,128)S(1)}, u32[]{:S(2)}, u32[]{:S(2)}) collective-permute-start(f32[392,128]{1,0:T(8,128)S(1)} %get-tuple-element.28), channel_id=1, source_target_pairs={{0,7},{1,0},{2,1},{3,2},{4,3},{5,4},{6,5},{7,6},{8,15},{9,8},{10,9... | collective-permute-start | bytes 602120 | tf_op jit(solution)/shard_map/ppermute | solution.py:538
  16.8 0.0 collective-permute-start.2
  16.8 5.1 %collective-permute-done.refs_1_ = f32[328,128]{1,0:T(8,128)S(1)} collective-permute-done((f32[328,128]{1,0:T(8,128)S(1)}, f32[328,128]{1,0:T(8,128)S(1)}, u32[]{:S(2)}, u32[]{:S(2)}) %collective-permute-start) | collective-permute-done | bytes 167968 | tf_op jit(solution)/shard_map/ppermute | solution.py:538
  21.9 0.0 collective-permute-start.3
  21.9 11.0 %collective-permute-done.1.refs_2_ = f32[328,128]{1,0:T(8,128)S(1)} collective-permute-done((f32[328,128]{1,0:T(8,128)S(1)}, f32[328,128]{1,0:T(8,128)S(1)}, u32[]{:S(2)}, u32[]{:S(2)}) %collective-permute-start.1) | collective-permute-done | bytes 167968 | tf_op jit(solution)/shard_map/ppermute | solution.py:538
  32.9 0.0 collective-permute-start.4
  33.5 3.7 %collective-permute-done.2.refs_3_ = f32[328,128]{1,0:T(8,128)S(1)} collective-permute-done((f32[328,128]{1,0:T(8,128)S(1)}, f32[328,128]{1,0:T(8,128)S(1)}, u32[]{:S(2)}, u32[]{:S(2)}) %collective-permute-start.2) | collective-permute-done | bytes 167968 | tf_op jit(solution)/shard_map/ppermute | solution.py:538
  37.2 0.0 collective-permute-done.3.refs_4_
  37.2 1.5 %collective-permute-done.4.refs_5_ = f32[328,128]{1,0:T(8,128)S(1)} collective-permute-done((f32[328,128]{1,0:T(8,128)S(1)}, f32[328,128]{1,0:T(8,128)S(1)}, u32[]{:S(2)}, u32[]{:S(2)}) %collective-permute-start.4) | collective-permute-done | bytes 167968 | tf_op jit(solution)/shard_map/ppermute | solution.py:538
  38.8 0.0 collective-permute-done.5.refs_6_
  38.8 0.0 collective-permute-done.6.refs_7_
  38.8 0.0 copy-done.5
  38.8 0.0 copy-done
  38.8 0.0 copy-done.7
  38.8 0.0 copy-done.6
  38.8 0.0 copy-start.1
  38.8 0.0 copy-start.2
  38.8 0.0 copy-start.3
  38.9 3.9 %shard_map.132 = (f32[192,128]{1,0:T(8,128)S(1)}, f32[192,128]{1,0:T(8,128)S(1)}, f32[192,128]{1,0:T(8,128)S(1)}, f32[192,128]{1,0:T(8,128)S(1)}, f32[192,128]{1...) custom-call(s32[1]{0:T(128)S(6)} %copy.14.offsets, ...), custom_call_target="tpu_custom_call" | custom-call | tf_op jit(solution)/shard_map/pallas_call | solution.py:488
  42.8 1.5 %collective-permute-start.14 = (f32[704,128]{1,0:T(8,128)S(1)}, f32[704,128]{1,0:T(8,128)S(1)}, u32[]{:S(2)}, u32[]{:S(2)}) collective-permute-start(f32[704,128]{1,0:T(8,128)S(1)} %get-tuple-element.39), channel_id=1, source_target_pairs={{0,8},{8,0},{1,9},{9,1},{2,10},{10,2},{3,11},{11,3},{4,12},{12,4},... | collective-permute-start | bytes 1081352 | tf_op jit(solution)/shard_map/ppermute | solution.py:538
  44.3 6.5 %collective-permute-start.7 = (f32[192,128]{1,0:T(8,128)S(1)}, f32[192,128]{1,0:T(8,128)S(1)}, u32[]{:S(2)}, u32[]{:S(2)}) collective-permute-start(f32[192,128]{1,0:T(8,128)S(1)} %get-tuple-element.30), channel_id=1, source_target_pairs={{0,5},{1,6},{2,7},{3,3},{4,4},{5,0},{6,1},{7,2},{8,13},{9,14},{10,... | collective-permute-start | bytes 294920 | tf_op jit(solution)/shard_map/ppermute | solution.py:538
  50.8 0.4 collective-permute-start.8
  51.2 1.9 %collective-permute-start.9 = (f32[192,128]{1,0:T(8,128)S(1)}, f32[192,128]{1,0:T(8,128)S(1)}, u32[]{:S(2)}, u32[]{:S(2)}) collective-permute-start(f32[192,128]{1,0:T(8,128)S(1)} %get-tuple-element.32), channel_id=1, source_target_pairs={{0,7},{1,3},{2,5},{3,6},{4,1},{5,2},{6,4},{7,0},{8,15},{9,11},{10,... | collective-permute-start | bytes 294920 | tf_op jit(solution)/shard_map/ppermute | solution.py:538
  53.1 0.0 collective-permute-start.10
  53.1 7.0 %collective-permute-done.7.refs_1_ = f32[192,128]{1,0:T(8,128)S(1)} collective-permute-done((f32[192,128]{1,0:T(8,128)S(1)}, f32[192,128]{1,0:T(8,128)S(1)}, u32[]{:S(2)}, u32[]{:S(2)}) %collective-permute-start.7) | collective-permute-done | bytes 98336 | tf_op jit(solution)/shard_map/ppermute | solution.py:538
  60.1 0.0 collective-permute-start.11
  60.1 0.0 collective-permute-done.8.refs_2_
  60.1 0.0 collective-permute-start.12
  60.1 0.0 collective-permute-done.9.refs_3_
  60.1 2.9 %collective-permute-start.13 = (f32[192,128]{1,0:T(8,128)S(1)}, f32[192,128]{1,0:T(8,128)S(1)}, u32[]{:S(2)}, u32[]{:S(2)}) collective-permute-start(f32[192,128]{1,0:T(8,128)S(1)} %get-tuple-element.36), channel_id=1, source_target_pairs={{0,3},{1,0},{2,1},{3,2},{4,5},{5,6},{6,7},{7,4},{8,11},{9,8},{10,9... | collective-permute-start | bytes 294920 | tf_op jit(solution)/shard_map/ppermute | solution.py:538
  63.0 0.0 collective-permute-done.10.refs_4_
  63.0 1.7 %collective-permute-done.11.refs_5_ = f32[192,128]{1,0:T(8,128)S(1)} collective-permute-done((f32[192,128]{1,0:T(8,128)S(1)}, f32[192,128]{1,0:T(8,128)S(1)}, u32[]{:S(2)}, u32[]{:S(2)}) %collective-permute-start.11) | collective-permute-done | bytes 98336 | tf_op jit(solution)/shard_map/ppermute | solution.py:538
  64.7 1.6 %collective-permute-done.12.refs_6_ = f32[192,128]{1,0:T(8,128)S(1)} collective-permute-done((f32[192,128]{1,0:T(8,128)S(1)}, f32[192,128]{1,0:T(8,128)S(1)}, u32[]{:S(2)}, u32[]{:S(2)}) %collective-permute-start.12) | collective-permute-done | bytes 98336 | tf_op jit(solution)/shard_map/ppermute | solution.py:538
  66.3 1.4 %collective-permute-done.13.refs_7_ = f32[192,128]{1,0:T(8,128)S(1)} collective-permute-done((f32[192,128]{1,0:T(8,128)S(1)}, f32[192,128]{1,0:T(8,128)S(1)}, u32[]{:S(2)}, u32[]{:S(2)}) %collective-permute-start.13) | collective-permute-done | bytes 98336 | tf_op jit(solution)/shard_map/ppermute | solution.py:538
  67.7 0.0 copy-start.8
  67.7 0.0 copy-start.9
  67.7 0.0 copy-start.10
  67.8 3.1 %shard_map.133 = f32[3,2,1,64,512]{4,3,2,1,0:T(8,128)} custom-call(s32[2,8,8]{2,1,0:T(8,128)S(1)} %copy-done.6, f32[192,128]{1,0:T(8,128)S(1)} %get-tuple-element.29.refs_0_, f32[192,128]{1,0:T(8,128)S(1)} %collective-permute-done.7.refs_1_, f32[192,128]{1,0:T(8,128)S(1)} %collective-permute-done.8.refs_2_, f32[192,128]{1,0:T(8,128)S(1)} %collective-permute-done.9.refs_3_, ...), custom_call_target="tpu_custom_call" | custom-call | tf_op jit(solution)/shard_map/pallas_call | solution.py:488
  70.8 0.0 collective-permute-done.14.refs_3_
  70.9 3.6 %shard_map.134 = f32[2,128,512]{2,1,0:T(8,128)} custom-call(f32[2,128,512]{2,1,0:T(8,128)S(1)} %copy-done, f32[2,8,512]{2,1,0:T(8,128)S(1)} %get-tuple-element.37.refs_1_, f32[704,128]{1,0:T(8,128)S(1)} %get-tuple-element.38.refs_2_, f32[704,128]{1,0:T(8,128)S(1)} %collective-permute-done.14.refs_3_, bf16[136,72]{1,0:T(8,128)(2,1)S(1)} %copy-done.10, ...), custom_call_target="tpu_custom_call" | custom-call | flops 4000000000 | tf_op jit(solution)/shard_map/pallas_call | solution.py:488
  (8 shorter events, 0.0 us)
Async XLA Ops:
  0.6 38.1 %copy-start.4 = (bf16[1024,512]{1,0:T(8,128)(2,1)S(1)}, bf16[1024,512]{1,0:T(8,128)(2,1)}, u32[]{:S(2)}) copy-start(bf16[1024,512]{1,0:T(8,128)(2,1)} %constant.23.clone.refs_11_) | copy-start | bytes 3145732
  0.6 38.1 %copy-start.5 = (bf16[1024,512]{1,0:T(8,128)(2,1)S(1)}, bf16[1024,512]{1,0:T(8,128)(2,1)}, u32[]{:S(2)}) copy-start(bf16[1024,512]{1,0:T(8,128)(2,1)} %constant.22.clone.refs_10_) | copy-start | bytes 3145732
  0.7 38.1 %copy-start = (f32[2,128,512]{2,1,0:T(8,128)S(1)}, f32[2,128,512]{2,1,0:T(8,128)}, u32[]{:S(2)}) copy-start(f32[2,128,512]{2,1,0:T(8,128)} %refs_0_.1) | copy-start | bytes 1572868
  5.4 33.4 %copy-start.7 = (s32[2,8,8]{2,1,0:T(8,128)S(1)}, s32[2,8,8]{2,1,0:T(8,128)}, u32[]{:S(2)}) copy-start(s32[2,8,8]{2,1,0:T(8,128)} %constant.18.clone.arrivals) | copy-start | bytes 1540
  5.4 33.4 %copy-start.6 = (s32[2,8,8]{2,1,0:T(8,128)S(1)}, s32[2,8,8]{2,1,0:T(8,128)}, u32[]{:S(2)}) copy-start(s32[2,8,8]{2,1,0:T(8,128)} %constant.19.clone.departures) | copy-start | bytes 1540
  5.4 16.5 %collective-permute-start = (f32[328,128]{1,0:T(8,128)S(1)}, f32[328,128]{1,0:T(8,128)S(1)}, u32[]{:S(2)}, u32[]{:S(2)}) collective-permute-start(f32[328,128]{1,0:T(8,128)S(1)} %get-tuple-element.22), channel_id=1, source_target_pairs={{0,4},{1,5},{2,6},{3,7},{4,0},{5,1},{6,2},{7,3},{8,12},{9,13},{10,... | collective-permute-start | bytes 503816 | tf_op jit(solution)/shard_map/ppermute | solution.py:538
  9.5 23.3 %collective-permute-start.1 = (f32[328,128]{1,0:T(8,128)S(1)}, f32[328,128]{1,0:T(8,128)S(1)}, u32[]{:S(2)}, u32[]{:S(2)}) collective-permute-start(f32[328,128]{1,0:T(8,128)S(1)} %get-tuple-element.23), channel_id=1, source_target_pairs={{0,3},{1,4},{2,5},{3,6},{4,7},{5,0},{6,1},{7,2},{8,11},{9,12},{10,... | collective-permute-start | bytes 503816 | tf_op jit(solution)/shard_map/ppermute | solution.py:538
  12.1 26.7 %collective-permute-start.5 = (f32[392,128]{1,0:T(8,128)S(1)}, f32[392,128]{1,0:T(8,128)S(1)}, u32[]{:S(2)}, u32[]{:S(2)}) collective-permute-start(f32[392,128]{1,0:T(8,128)S(1)} %get-tuple-element.27), channel_id=1, source_target_pairs={{0,1},{1,2},{2,3},{3,4},{4,5},{5,6},{6,7},{7,0},{8,9},{9,10},{10,1... | collective-permute-start | bytes 602120 | tf_op jit(solution)/shard_map/ppermute | solution.py:538
  12.1 26.7 %collective-permute-start.6 = (f32[392,128]{1,0:T(8,128)S(1)}, f32[392,128]{1,0:T(8,128)S(1)}, u32[]{:S(2)}, u32[]{:S(2)}) collective-permute-start(f32[392,128]{1,0:T(8,128)S(1)} %get-tuple-element.28), channel_id=1, source_target_pairs={{0,7},{1,0},{2,1},{3,2},{4,3},{5,4},{6,5},{7,6},{8,15},{9,8},{10,9... | collective-permute-start | bytes 602120 | tf_op jit(solution)/shard_map/ppermute | solution.py:538
  16.8 20.4 %collective-permute-start.2 = (f32[328,128]{1,0:T(8,128)S(1)}, f32[328,128]{1,0:T(8,128)S(1)}, u32[]{:S(2)}, u32[]{:S(2)}) collective-permute-start(f32[328,128]{1,0:T(8,128)S(1)} %get-tuple-element.24), channel_id=1, source_target_pairs={{0,5},{1,6},{2,7},{3,0},{4,1},{5,2},{6,3},{7,4},{8,13},{9,14},{10,... | collective-permute-start | bytes 503816 | tf_op jit(solution)/shard_map/ppermute | solution.py:538
  21.9 15.3 %collective-permute-start.3 = (f32[328,128]{1,0:T(8,128)S(1)}, f32[328,128]{1,0:T(8,128)S(1)}, u32[]{:S(2)}, u32[]{:S(2)}) collective-permute-start(f32[328,128]{1,0:T(8,128)S(1)} %get-tuple-element.25), channel_id=1, source_target_pairs={{0,2},{1,3},{2,4},{3,5},{4,6},{5,7},{6,0},{7,1},{8,10},{9,11},{10,... | collective-permute-start | bytes 503816 | tf_op jit(solution)/shard_map/ppermute | solution.py:538
  32.9 5.9 %collective-permute-start.4 = (f32[328,128]{1,0:T(8,128)S(1)}, f32[328,128]{1,0:T(8,128)S(1)}, u32[]{:S(2)}, u32[]{:S(2)}) collective-permute-start(f32[328,128]{1,0:T(8,128)S(1)} %get-tuple-element.26), channel_id=1, source_target_pairs={{0,6},{1,7},{2,0},{3,1},{4,2},{5,3},{6,4},{7,5},{8,14},{9,15},{10,... | collective-permute-start | bytes 503816 | tf_op jit(solution)/shard_map/ppermute | solution.py:538
  38.8 28.9 %copy-start.1 = (bf16[512,1024]{1,0:T(8,128)(2,1)S(1)}, bf16[512,1024]{1,0:T(8,128)(2,1)}, u32[]{:S(2)}) copy-start(bf16[512,1024]{1,0:T(8,128)(2,1)} %constant.21.clone.low_in.refs_10_) | copy-start | bytes 3145732
  38.8 28.9 %copy-start.2 = (bf16[512,1024]{1,0:T(8,128)(2,1)S(1)}, bf16[512,1024]{1,0:T(8,128)(2,1)}, u32[]{:S(2)}) copy-start(bf16[512,1024]{1,0:T(8,128)(2,1)} %constant.20.clone.high_in.refs_9_) | copy-start | bytes 3145732
  38.8 28.9 %copy-start.3 = (f32[3,2,1,64,512]{4,3,2,1,0:T(8,128)S(1)}, f32[3,2,1,64,512]{4,3,2,1,0:T(8,128)}, u32[]{:S(2)}) copy-start(f32[3,2,1,64,512]{4,3,2,1,0:T(8,128)} %refs_8_.3) | copy-start | bytes 2359300
  42.8 28.1 %collective-permute-start.14 = (f32[704,128]{1,0:T(8,128)S(1)}, f32[704,128]{1,0:T(8,128)S(1)}, u32[]{:S(2)}, u32[]{:S(2)}) collective-permute-start(f32[704,128]{1,0:T(8,128)S(1)} %get-tuple-element.39), channel_id=1, source_target_pairs={{0,8},{8,0},{1,9},{9,1},{2,10},{10,2},{3,11},{11,3},{4,12},{12,4},... | collective-permute-start | bytes 1081352 | tf_op jit(solution)/shard_map/ppermute | solution.py:538
  44.3 15.8 %collective-permute-start.7 = (f32[192,128]{1,0:T(8,128)S(1)}, f32[192,128]{1,0:T(8,128)S(1)}, u32[]{:S(2)}, u32[]{:S(2)}) collective-permute-start(f32[192,128]{1,0:T(8,128)S(1)} %get-tuple-element.30), channel_id=1, source_target_pairs={{0,5},{1,6},{2,7},{3,3},{4,4},{5,0},{6,1},{7,2},{8,13},{9,14},{10,... | collective-permute-start | bytes 294920 | tf_op jit(solution)/shard_map/ppermute | solution.py:538
  50.8 9.3 %collective-permute-start.8 = (f32[192,128]{1,0:T(8,128)S(1)}, f32[192,128]{1,0:T(8,128)S(1)}, u32[]{:S(2)}, u32[]{:S(2)}) collective-permute-start(f32[192,128]{1,0:T(8,128)S(1)} %get-tuple-element.31), channel_id=1, source_target_pairs={{0,6},{1,5},{2,3},{3,7},{4,0},{5,4},{6,2},{7,1},{8,14},{9,13},{10,... | collective-permute-start | bytes 294920 | tf_op jit(solution)/shard_map/ppermute | solution.py:538
  51.2 8.8 %collective-permute-start.9 = (f32[192,128]{1,0:T(8,128)S(1)}, f32[192,128]{1,0:T(8,128)S(1)}, u32[]{:S(2)}, u32[]{:S(2)}) collective-permute-start(f32[192,128]{1,0:T(8,128)S(1)} %get-tuple-element.32), channel_id=1, source_target_pairs={{0,7},{1,3},{2,5},{3,6},{4,1},{5,2},{6,4},{7,0},{8,15},{9,11},{10,... | collective-permute-start | bytes 294920 | tf_op jit(solution)/shard_map/ppermute | solution.py:538
  53.1 9.9 %collective-permute-start.10 = (f32[192,128]{1,0:T(8,128)S(1)}, f32[192,128]{1,0:T(8,128)S(1)}, u32[]{:S(2)}, u32[]{:S(2)}) collective-permute-start(f32[192,128]{1,0:T(8,128)S(1)} %get-tuple-element.33), channel_id=1, source_target_pairs={{0,3},{1,7},{2,6},{3,5},{4,2},{5,1},{6,0},{7,4},{8,11},{9,15},{10,... | collective-permute-start | bytes 294920 | tf_op jit(solution)/shard_map/ppermute | solution.py:538
  60.1 4.6 %collective-permute-start.11 = (f32[192,128]{1,0:T(8,128)S(1)}, f32[192,128]{1,0:T(8,128)S(1)}, u32[]{:S(2)}, u32[]{:S(2)}) collective-permute-start(f32[192,128]{1,0:T(8,128)S(1)} %get-tuple-element.34), channel_id=1, source_target_pairs={{0,2},{1,3},{2,0},{3,1},{4,6},{5,7},{6,4},{7,5},{8,10},{9,11},{10,... | collective-permute-start | bytes 294920 | tf_op jit(solution)/shard_map/ppermute | solution.py:538
  60.1 6.2 %collective-permute-start.12 = (f32[192,128]{1,0:T(8,128)S(1)}, f32[192,128]{1,0:T(8,128)S(1)}, u32[]{:S(2)}, u32[]{:S(2)}) collective-permute-start(f32[192,128]{1,0:T(8,128)S(1)} %get-tuple-element.35), channel_id=1, source_target_pairs={{0,1},{1,2},{2,3},{3,0},{4,7},{5,4},{6,5},{7,6},{8,9},{9,10},{10,1... | collective-permute-start | bytes 294920 | tf_op jit(solution)/shard_map/ppermute | solution.py:538
  60.1 7.6 %collective-permute-start.13 = (f32[192,128]{1,0:T(8,128)S(1)}, f32[192,128]{1,0:T(8,128)S(1)}, u32[]{:S(2)}, u32[]{:S(2)}) collective-permute-start(f32[192,128]{1,0:T(8,128)S(1)} %get-tuple-element.36), channel_id=1, source_target_pairs={{0,3},{1,0},{2,1},{3,2},{4,5},{5,6},{6,7},{7,4},{8,11},{9,8},{10,9... | collective-permute-start | bytes 294920 | tf_op jit(solution)/shard_map/ppermute | solution.py:538
  67.7 3.1 %copy-start.8 = (bf16[384,640]{1,0:T(8,128)(2,1)S(1)}, bf16[384,640]{1,0:T(8,128)(2,1)}, u32[]{:S(2)}) copy-start(bf16[384,640]{1,0:T(8,128)(2,1)} %constant.26.clone.refs_6_) | copy-start | bytes 1474564
  67.7 3.1 %copy-start.9 = (bf16[136,72]{1,0:T(8,128)(2,1)S(1)}, bf16[136,72]{1,0:T(8,128)(2,1)}, u32[]{:S(2)}) copy-start(bf16[136,72]{1,0:T(8,128)(2,1)} %constant.25.clone.refs_5_) | copy-start | bytes 58756
  67.7 3.1 %copy-start.10 = (bf16[136,72]{1,0:T(8,128)(2,1)S(1)}, bf16[136,72]{1,0:T(8,128)(2,1)}, u32[]{:S(2)}) copy-start(bf16[136,72]{1,0:T(8,128)(2,1)} %constant.24.clone.refs_4_) | copy-start | bytes 58756
